TPU v7x, 8 devices: a whole 2x2x1 slice. The times are simulated.
8 devices in a mesh: dp: 1 (over z), sp: 8 (over y, x, core).
Axes of the slice: x: 2, y: 2, z: 1, core: 2. Of those that a mesh axis runs over, the one named last changes fastest.
Arguments:
- spec_tok: bfloat16 [64, 5, 1536], P('dp')
- patch_tok: bfloat16 [64, 256, 1536], P('dp', 'sp')
- norm1_w: bfloat16 [1536], replicated
- norm1_b: bfloat16 [1536], replicated
- w_qkv: bfloat16 [1536, 4608], replicated
- b_qkv: bfloat16 [4608], replicated
- w_out: bfloat16 [24, 64, 1536], replicated
- b_out: bfloat16 [1536], replicated
- scale_attn: bfloat16 [1536], replicated
- norm2_w: bfloat16 [1536], replicated
- norm2_b: bfloat16 [1536], replicated
- w_gate: bfloat16 [1536, 4096], replicated
- b_gate: bfloat16 [4096], replicated
- w_up: bfloat16 [1536, 4096], replicated
- b_up: bfloat16 [4096], replicated
- w_down: bfloat16 [4096, 1536], replicated
- b_down: bfloat16 [1536], replicated
- scale_mlp: bfloat16 [1536], replicated
- dy_spec: bfloat16 [64, 5, 1536], P('dp')
- dy_patch: bfloat16 [64, 256, 1536], P('dp', 'sp')
Outputs:
- output 1: bfloat16 [64, 5, 1536], P('dp')
- output 2: bfloat16 [64, 256, 1536], P('dp', 'sp')
- output 3: bfloat16 [64, 5, 1536], P('dp')
- output 4: bfloat16 [64, 256, 1536], P('dp', 'sp')
- output 5: float32 [1536], P('dp')
- output 6: float32 [1536], P('dp')
- output 7: float32 [1536, 4608], P('dp')
- output 8: float32 [4608], P('dp')
- output 9: float32 [24, 64, 1536], P('dp')
- output 10: float32 [1536], P('dp')
- output 11: float32 [1536], P('dp')
- output 12: float32 [1536], P('dp')
- output 13: float32 [1536], P('dp')
- output 14: float32 [1536, 4096], P('dp')
- output 15: float32 [4096], P('dp')
- output 16: float32 [1536, 4096], P('dp')
- output 17: float32 [4096], P('dp')
- output 18: float32 [4096, 1536], P('dp')
- output 19: float32 [1536], P('dp')
- output 20: float32 [1536], P('dp')
All inputs are finite; a program needn't handle non-finite values.
Results may differ from a plain program's by a relative error of at most 0.0173021.
Values are sent between devices in bfloat16 or wider.
A program may use at most 1 GiB of HBM per device.

v0:
```python
import jax
import jax.numpy as jnp
from jax import lax
from jax.sharding import PartitionSpec as P

NORM_EPS = 1e-6
SPECIAL = 5


def norm_forward(tok_f32, weight, bias):
    row_mean = jnp.mean(tok_f32, axis=-1, keepdims=True)
    centred = tok_f32 - row_mean
    inv_std = lax.rsqrt(jnp.mean(centred * centred, axis=-1, keepdims=True) + NORM_EPS)
    norm_hat = centred * inv_std
    normed = (norm_hat * weight.astype(jnp.float32) + bias.astype(jnp.float32)).astype(jnp.bfloat16)
    return norm_hat, inv_std, normed


def norm_backward(d_normed, norm_hat, inv_std, weight):
    d_hat = d_normed * weight.astype(jnp.float32)
    mean_grad = jnp.mean(d_hat, axis=-1, keepdims=True)
    mean_proj = jnp.mean(d_hat * norm_hat, axis=-1, keepdims=True)
    return inv_std * (d_hat - mean_grad - norm_hat * mean_proj)


def row_sum(values, row_weight):
    return jnp.einsum("btf,t->f", values, row_weight, preferred_element_type=jnp.float32)


def solution(mesh):
    groups = mesh.shape["sp"]
    tok_spec = P("dp", None, None)
    seq_spec = P("dp", "sp", None)
    shared = P()
    vec_spec = P("dp")
    mat_spec = P("dp", None)

    def local_block(spec_tok, patch_tok, norm1_w, norm1_b, w_qkv, b_qkv, w_out, b_out, scale_attn,
                    norm2_w, norm2_b, w_gate, b_gate, w_up, b_up, w_down, b_down, scale_mlp,
                    dy_spec, dy_patch):
        num_heads, head_dim, model_width = w_out.shape
        local_heads = num_heads // groups
        batch_size, local_patch = patch_tok.shape[0], patch_tok.shape[1]
        local_len = SPECIAL + local_patch
        sp_rank = lax.axis_index("sp")
        first_dev = (sp_rank == 0).astype(jnp.float32)
        row_weight = jnp.concatenate([jnp.full((SPECIAL,), first_dev), jnp.ones((local_patch,), jnp.float32)])
        row_half = row_weight.astype(jnp.bfloat16)
        row_col = row_half[:, None]
        attn_scale = head_dim ** -0.5

        def to_heads(local_arr, head_axis):
            spec_part = lax.dynamic_slice_in_dim(local_arr[:, :SPECIAL], sp_rank * local_heads, local_heads, axis=head_axis)
            patch_part = lax.all_to_all(local_arr[:, SPECIAL:], "sp", head_axis, 1, tiled=True)
            return jnp.concatenate([spec_part, patch_part], axis=1)

        def from_heads(head_arr, head_axis):
            spec_part = lax.all_gather(head_arr[:, :SPECIAL], "sp", axis=head_axis, tiled=True)
            patch_part = lax.all_to_all(head_arr[:, SPECIAL:], "sp", 1, head_axis, tiled=True)
            return jnp.concatenate([spec_part, patch_part], axis=1)

        tok_f32 = jnp.concatenate([spec_tok, patch_tok], axis=1).astype(jnp.float32)
        norm_hat1, inv_std1, normed1 = norm_forward(tok_f32, norm1_w, norm1_b)
        qkv_local = (jnp.einsum("btd,de->bte", normed1, w_qkv, preferred_element_type=jnp.float32)
                     + b_qkv.astype(jnp.float32)).astype(jnp.bfloat16)
        qkv_heads = to_heads(qkv_local.reshape(batch_size, local_len, 3, num_heads, head_dim), 3)
        queries = qkv_heads[:, :, 0]
        key_vecs = qkv_heads[:, :, 1]
        values = qkv_heads[:, :, 2]
        scores = jnp.einsum("bqhd,bkhd->bhqk", queries, key_vecs, preferred_element_type=jnp.float32) * attn_scale
        attn_probs = jax.nn.softmax(scores, axis=-1)
        probs_half = attn_probs.astype(jnp.bfloat16)
        context = jnp.einsum("bhqk,bkhd->bqhd", probs_half, values, preferred_element_type=jnp.float32).astype(jnp.bfloat16)
        ctx_local = from_heads(context, 2)
        branch1 = jnp.einsum("bthd,hde->bte", ctx_local, w_out, preferred_element_type=jnp.float32) + b_out.astype(jnp.float32)
        resid_f32 = (tok_f32 + scale_attn.astype(jnp.float32) * branch1).astype(jnp.bfloat16).astype(jnp.float32)
        norm_hat2, inv_std2, normed2 = norm_forward(resid_f32, norm2_w, norm2_b)
        gate_pre = jnp.einsum("btd,df->btf", normed2, w_gate, preferred_element_type=jnp.float32) + b_gate.astype(jnp.float32)
        up_proj = jnp.einsum("btd,df->btf", normed2, w_up, preferred_element_type=jnp.float32) + b_up.astype(jnp.float32)
        gate_sig = jax.nn.sigmoid(gate_pre)
        gate_act = gate_pre * gate_sig
        hidden = (gate_act * up_proj).astype(jnp.bfloat16)
        branch2 = jnp.einsum("btf,fd->btd", hidden, w_down, preferred_element_type=jnp.float32) + b_down.astype(jnp.float32)
        block_out = (resid_f32 + scale_mlp.astype(jnp.float32) * branch2).astype(jnp.bfloat16)

        d_out = jnp.concatenate([dy_spec, dy_patch], axis=1).astype(jnp.float32)
        g_scale_mlp = row_sum(d_out * branch2, row_weight)
        d_branch2 = d_out * scale_mlp.astype(jnp.float32)
        g_b_down = row_sum(d_branch2, row_weight)
        d_branch2_h = d_branch2.astype(jnp.bfloat16)
        g_w_down = jnp.einsum("btf,btd->fd", hidden, d_branch2_h * row_col, preferred_element_type=jnp.float32)
        d_hidden = jnp.einsum("btd,fd->btf", d_branch2_h, w_down, preferred_element_type=jnp.float32)
        d_up = d_hidden * gate_act
        d_gate = d_hidden * up_proj * gate_sig * (1.0 + gate_pre * (1.0 - gate_sig))
        g_b_gate = row_sum(d_gate, row_weight)
        g_b_up = row_sum(d_up, row_weight)
        d_gate_h = d_gate.astype(jnp.bfloat16)
        d_up_h = d_up.astype(jnp.bfloat16)
        g_w_gate = jnp.einsum("btd,btf->df", normed2, d_gate_h * row_col, preferred_element_type=jnp.float32)
        g_w_up = jnp.einsum("btd,btf->df", normed2, d_up_h * row_col, preferred_element_type=jnp.float32)
        d_normed2 = (jnp.einsum("btf,df->btd", d_gate_h, w_gate, preferred_element_type=jnp.float32)
                     + jnp.einsum("btf,df->btd", d_up_h, w_up, preferred_element_type=jnp.float32))
        g_norm2_w = row_sum(d_normed2 * norm_hat2, row_weight)
        g_norm2_b = row_sum(d_normed2, row_weight)
        d_resid = d_out + norm_backward(d_normed2, norm_hat2, inv_std2, norm2_w)
        g_scale_attn = row_sum(d_resid * branch1, row_weight)
        d_branch1 = d_resid * scale_attn.astype(jnp.float32)
        g_b_out = row_sum(d_branch1, row_weight)
        d_branch1_h = d_branch1.astype(jnp.bfloat16)
        g_w_out = jnp.einsum("bthd,bte->hde", ctx_local, d_branch1_h * row_col, preferred_element_type=jnp.float32)
        d_ctx = jnp.einsum("bte,hde->bthd", d_branch1_h, w_out, preferred_element_type=jnp.float32).astype(jnp.bfloat16)
        d_ctx_heads = to_heads(d_ctx, 2)
        d_values = jnp.einsum("bhqk,bqhd->bkhd", probs_half, d_ctx_heads, preferred_element_type=jnp.float32)
        d_probs = jnp.einsum("bqhd,bkhd->bhqk", d_ctx_heads, values, preferred_element_type=jnp.float32)
        d_scores = (attn_probs * (d_probs - jnp.sum(d_probs * attn_probs, axis=-1, keepdims=True))
                    * attn_scale).astype(jnp.bfloat16)
        d_queries = jnp.einsum("bhqk,bkhd->bqhd", d_scores, key_vecs, preferred_element_type=jnp.float32)
        d_keys = jnp.einsum("bhqk,bqhd->bkhd", d_scores, queries, preferred_element_type=jnp.float32)
        d_qkv_heads = jnp.stack([d_queries, d_keys, d_values], axis=2).astype(jnp.bfloat16)
        d_qkv = from_heads(d_qkv_heads, 3).reshape(batch_size, local_len, 3 * model_width)
        g_b_qkv = row_sum(d_qkv, row_half)
        g_w_qkv = jnp.einsum("btd,bte->de", normed1, d_qkv * row_col, preferred_element_type=jnp.float32)
        d_normed1 = jnp.einsum("bte,de->btd", d_qkv, w_qkv, preferred_element_type=jnp.float32)
        g_norm1_w = row_sum(d_normed1 * norm_hat1, row_weight)
        g_norm1_b = row_sum(d_normed1, row_weight)
        d_tokens = (d_resid + norm_backward(d_normed1, norm_hat1, inv_std1, norm1_w)).astype(jnp.bfloat16)
        all_grads = lax.psum((g_norm1_w, g_norm1_b, g_w_qkv, g_b_qkv, g_w_out, g_b_out, g_scale_attn,
                              g_norm2_w, g_norm2_b, g_w_gate, g_b_gate, g_w_up, g_b_up, g_w_down, g_b_down,
                              g_scale_mlp), "sp")
        return (block_out[:, :SPECIAL], block_out[:, SPECIAL:], d_tokens[:, :SPECIAL], d_tokens[:, SPECIAL:]) + all_grads

    in_specs = (tok_spec, seq_spec) + (shared,) * 16 + (tok_spec, seq_spec)
    out_specs = (tok_spec, seq_spec, tok_spec, seq_spec, vec_spec, vec_spec, mat_spec, vec_spec,
                 P("dp", None, None), vec_spec, vec_spec, vec_spec, vec_spec, mat_spec, vec_spec,
                 mat_spec, vec_spec, mat_spec, vec_spec, vec_spec)
    return jax.shard_map(local_block, mesh=mesh, in_specs=in_specs, out_specs=out_specs, check_vma=False)
```

profile of v0, /device:TPU:1, one launch (start us, length us, event | category | flops | bytes accessed | tf_op | source)
XLA Modules:
  0.0 4112.1 jit_solution(9255030754356393769)
XLA Ops:
  20.3 40.0 add_convert_fusion
  60.3 52.9 %reshape.102 = bf16[64,37,3,24,64]{4,3,2,0,1:T(8,128)(2,1)} reshape(bf16[64,37,4608]{2,0,1:T(8,128)(2,1)} %add_convert_fusion) | data formatting | bytes 43646976 | tf_op jit(solution)/shard_map/reshape | solution.py:66
  113.2 25.8 slice.61
  139.0 34.2 copy.151
  173.2 59.3 %reshape.148 = bf16[8,2,589824]{2,1,0:T(2,128)(2,1)} reshape(bf16[24,64,3,32,64]{4,3,2,1,0:T(8,128)(2,1)} %bitcast.182) | data formatting | bytes 37748736
  246.5 6.7 copy.147
  253.3 187.1 %all-to-all-done = bf16[8,2,589824]{2,1,0:T(2,128)(2,1)} async-done(((bf16[8,2,589824]{2,1,0:T(2,128)(2,1)}), bf16[8,2,589824]{2,1,0:T(2,128)(2,1)}, u32[]{:S(2)}, u32[]{:S(2)}) %all-to-all-start) | async-done | bytes 18874400 | tf_op jit(solution)/shard_map/all_to_all | solution.py:54
  440.4 58.4 %reshape.149 = bf16[24,64,3,32,64]{4,3,2,1,0:T(8,128)(2,1)} reshape(bf16[8,2,589824]{2,1,0:T(2,128)(2,1)} %all-to-all-done) | data formatting | bytes 37748736
  498.8 25.9 copy.110
  524.8 34.1 copy.111
  558.8 18.6 fusion.92
  577.4 37.0 fusion.147
  614.5 34.1 convert_bitcast_fusion.3
  648.6 9.7 slice.67
  658.3 18.5 copy.113
  676.8 13.8 reshape.150
  690.6 8.1 all-to-all-start.1
  698.8 9.0 copy.117
  710.2 217.7 %all_gather.6 = bf16[64,5,24,64]{1,3,2,0:T(8,128)(2,1)} all-gather(bf16[64,5,3,64]{1,3,2,0:T(8,128)(2,1)S(1)} %slice-done.14), channel_id=1, replica_groups=mesh['dp'=1,'sp'=8] {'sp'}, dimensions={2}, use_global_device_ids=true | all-gather | bytes 1105920 | tf_op jit(solution)/shard_map/all_gather | solution.py:58
  927.8 21.8 copy.116
  949.6 13.3 reshape.151
  962.9 12.7 copy.115
  975.6 25.3 convert_reduce_fusion.1
  1006.3 39.8 fusion.77
  1046.3 37.3 fusion.81
  1083.5 77.6 %multiply_reduce_fusion.2 = (bf16[37,4096]{1,0:T(8,128)(2,1)}, bf16[64,37,4096]{2,0,1:T(8,128)(2,1)}, bf16[64,37,4096]{2,0,1:T(8,128)(2,1)}, bf16[37,4096]{1,0:T(8,128)(2,1)}, bf16[64,37,4096]{2,0,1:T(8,128)(2,1)}) fusion(f32[64,37,4096]{2,0,1:T(8,128)} %fusion.81, f32[4096]{0:T(1024)S(1)} %copy-done.30, f32[64,37,4096]{2,0,1:T(8,128)} %fusion.77, ...), kind=kOutput, calls=%fused_computation.61 | convolution fusion | flops 29994868736 | bytes 156293120 | tf_op jit(solution)/shard_map/btd,fd->btf/dot_general | solution.py:92
  1161.1 39.0 fusion.75
  1200.2 49.6 %fusion.54 = (bf16[37,1536]{1,0:T(8,128)(2,1)}, f32[64,37]{0,1:T(8,128)S(1)}, f32[64,37]{0,1:T(8,128)S(1)}, bf16[37,1536]{1,0:T(8,128)(2,1)}, f32[64,37,1536]{2,0,1:T(8,128)}) fusion(bf16[64,37,1536]{2,0,1:T(8,128)(2,1)} %get-tuple-element.132, f32[64,37]{0,1:T(8,128)S(1)} %copy-done.27, f32[64,37]{0,1:T(8,128)S(1)} %copy-done.19, f32[1536]{0:T(1024)S(1)} %copy-done.43, ...), kind=kOutput, calls=%fused_computation.68 | convolution fusion | flops 29836226560 | bytes 68625408 | tf_op jit(solution)/shard_map/btf,df->btd/dot_general | solution.py:101
  1249.8 55.1 %fusion.67 = (bf16[37,1536]{1,0:T(8,128)(2,1)}, bf16[37,1536]{1,0:T(8,128)(2,1)}, bf16[64,37,1536]{2,0,1:T(8,128)(2,1)}, bf16[37,1536]{1,0:T(8,128)(2,1)}, bf16[...) fusion(f32[1536]{0:T(1024)S(1)} %copy-done.52, bf16[64,32,1536]{2,0,1:T(8,128)(2,1)} %copy.117, ...), kind=kOutput, calls=%fused_computation.81 | convolution fusion | flops 29890674688 | bytes 97975296 | tf_op jit(solution)/shard_map/btf,fd->btd/dot_general | solution.py:83
  1304.9 26.8 convolution_convert_fusion
  1342.0 14.1 reshape.152
  1367.5 61.3 %all-to-all-done.2 = bf16[8,2,196608]{2,1,0:T(2,128)(2,1)} async-done(((bf16[8,2,196608]{2,1,0:T(2,128)(2,1)}), bf16[8,2,196608]{2,1,0:T(2,128)(2,1)}, u32[]{:S(2)}, u32[]{:S(2)}) %all-to-all-start.2) | async-done | bytes 6291488 | tf_op jit(solution)/shard_map/all_to_all | solution.py:54
  1428.8 13.3 reshape.153
  1442.2 13.4 copy.119
  1455.6 12.2 copy.121
  1467.8 33.8 fusion.116
  1501.6 99.5 %convert_bitcast_fusion.2 = bf16[64,261,1,3,64]{1,4,3,0,2:T(8,128)(2,1)} fusion(bf16[64,261,3,64]{1,3,2,0:T(8,128)(2,1)} %get-tuple-element.139, f32[64,3,261,261]{2,3,1,0:T(8,128)} %fusion.116, f32[64,3,261,261]{2,3,1,0:T(8,128)} %get-tuple-element.146, f32[64,3,261]{2,1,0:T(4,128)S(1)} %copy-done.73), kind=kOutput, calls=%fused_computation.120 | convolution fusion | flops 1768953856 | bytes 117662976 | tf_op jit(solution)/shard_map/bhqk,bkhd->bqhd/dot_general | solution.py:117
  1601.1 99.8 %convert_bitcast_fusion.1 = bf16[64,261,1,3,64]{1,4,3,0,2:T(8,128)(2,1)} fusion(bf16[64,261,3,64]{1,3,2,0:T(8,128)(2,1)} %get-tuple-element.140, f32[64,3,261,261]{2,3,1,0:T(8,128)} %fusion.116, f32[64,3,261,261]{2,3,1,0:T(8,128)} %get-tuple-element.146, f32[64,3,261]{2,1,0:T(4,128)S(1)} %copy-done.73), kind=kOutput, calls=%fused_computation.119 | convolution fusion | flops 1768953856 | bytes 117662976 | tf_op jit(solution)/shard_map/bhqk,bqhd->bkhd/dot_general | solution.py:118
  1700.9 32.5 convert_bitcast_fusion
  1733.4 22.9 pad_maximum_fusion
  1756.2 51.7 %copy.126 = bf16[64,256,3,3,64]{4,0,3,2,1:T(8,128)(2,1)} copy(bf16[64,256,3,3,64]{1,4,3,0,2:T(8,128)(2,1)} %pad_maximum_fusion) | data formatting | bytes 37748736 | tf_op jit(solution)/shard_map/slice | solution.py:59
  1808.0 59.4 %reshape.154 = bf16[8,2,589824]{2,1,0:T(2,128)(2,1)} reshape(bf16[256,3,3,64,64]{4,3,2,1,0:T(8,128)(2,1)} %bitcast.185) | data formatting | bytes 37748736
  1867.4 8.6 all-to-all-start.3
  1876.8 21.8 fusion.117
  1898.7 44.1 %fusion.46 = f32[1536,4096]{1,0:T(8,128)} fusion(bf16[64,37,4096]{2,0,1:T(8,128)(2,1)} %get-tuple-element.135, bf16[37]{0:T(256)(128)(2,1)S(1)} %copy-done.70, bf16[64,37,1536]{2,0,1:T(8,128)(2,1)} %get-tuple-element.132, f32[1536]{0:T(1024)S(1)} %copy-done.46, f32[1536]{0:T(1024)S(1)} %copy-done.44, f32[64,37]{0,1:T(8,128)S(1)} %copy-done.28, ...), kind=kOutput, calls=%fused_computation.60 | convolution fusion | flops 29827858432 | bytes 51870280 | tf_op jit(solution)/shard_map/btd,btf->df/dot_general | solution.py:100
  1942.8 44.3 %fusion.43 = f32[1536,4096]{1,0:T(8,128)} fusion(bf16[37]{0:T(256)(128)(2,1)S(1)} %copy-done.70, bf16[64,37,4096]{2,0,1:T(8,128)(2,1)} %get-tuple-element.138, bf16[64,37,1536]{2,0,1:T(8,128)(2,1)} %get-tuple-element.132, f32[1536]{0:T(1024)S(1)} %copy-done.46, f32[1536]{0:T(1024)S(1)} %copy-done.44, f32[64,37]{0,1:T(8,128)S(1)} %copy-done.28, ...), kind=kOutput, calls=%fused_computation.59 | convolution fusion | flops 29827858432 | bytes 51870280 | tf_op jit(solution)/shard_map/btd,btf->df/dot_general | solution.py:99
  1987.1 8.9 pad_maximum_fusion.3
  1999.1 42.0 %convolution_bitcast_fusion = f32[4096,1536]{1,0:T(8,128)} fusion(bf16[64,37,4096]{2,0,1:T(8,128)(2,1)} %get-tuple-element.136, f32[1536]{0:T(1024)S(1)} %copy-done.41, bf16[37]{0:T(256)(128)(2,1)S(1)} %copy-done.70, bf16[64,32,1536]{2,0,1:T(8,128)(2,1)} %copy.117, bf16[64,5,1536]{2,0,1:T(8,128)(2,1)S(1)} %copy-done.69), kind=kOutput, calls=%fused_computation.58 | convolution fusion | flops 29814521856 | bytes 51845192 | tf_op jit(solution)/shard_map/btf,btd->fd/dot_general | solution.py:91
  2041.1 354.6 %all-gather.2.cloned.1.call-done = bf16[64,5,3,24,64]{1,4,3,0,2:T(8,128)(2,1)} async-done(((bf16[64,5,3,3,64]{1,4,3,0,2:T(8,128)(2,1)}), bf16[64,5,3,24,64]{1,4,3,0,2:T(8,128)(2,1)}) %all-gather.2.cloned.1.call-update) | async-done | bytes 2949136 | tf_op jit(solution)/shard_map/all_gather | solution.py:58
  2395.7 58.9 %copy.125 = bf16[64,5,3,24,64]{4,3,2,0,1:T(8,128)(2,1)} copy(bf16[64,5,3,24,64]{1,4,3,0,2:T(8,128)(2,1)} %all-gather.2.cloned.1.call-done) | data formatting | bytes 5898240 | tf_op jit(solution)/shard_map/all_gather | solution.py:58
  2454.6 6.9 concatenate.31
  2463.5 58.6 %reshape.155 = bf16[256,3,3,64,64]{4,3,2,1,0:T(8,128)(2,1)} reshape(bf16[8,2,589824]{2,1,0:T(2,128)(2,1)} %all-to-all-done.3) | data formatting | bytes 37748736
  2522.1 49.6 %copy.144 = bf16[64,32,3,8,3,64]{5,4,3,2,0,1:T(4,128)(2,1)} copy(bf16[64,32,3,8,3,64]{5,0,4,2,1,3:T(8,128)(2,1)} %bitcast.186) | data formatting | bytes 37748736 | tf_op jit(solution)/shard_map/concatenate | solution.py:60
  2571.7 73.9 %reshape.138 = bf16[64,32,4608]{2,0,1:T(8,128)(2,1)} reshape(bf16[64,32,3,8,3,64]{5,4,3,2,0,1:T(4,128)(2,1)} %copy.144) | data formatting | bytes 37748736 | tf_op jit(solution)/shard_map/concatenate | solution.py:60
  2645.6 16.9 constant_dynamic-update-slice_fusion
  2662.5 51.4 %fusion.63 = (bf16[37,1536]{1,0:T(8,128)(2,1)S(1)}, f32[64,37]{0,1:T(8,128)S(1)}, f32[64,37]{0,1:T(8,128)S(1)}, bf16[37,1536]{1,0:T(8,128)(2,1)S(1)}, f32[64,37,1536]{2,0,1:T(8,128)}) fusion(f32[64,37]{0,1:T(8,128)S(1)} %copy-done.17, f32[64,37]{0,1:T(8,128)S(1)} %copy-done.12, bf16[64,32,1536]{2,0,1:T(8,128)(2,1)} %copy-done, ...), kind=kOutput, calls=%fused_computation.77 | convolution fusion | flops 33568043008 | bytes 58074112 | tf_op jit(solution)/shard_map/bte,de->btd/dot_general | solution.py:123
  2713.9 9.4 convert_reduce_fusion
  2725.7 49.1 %fusion.18 = f32[1536,4608]{1,0:T(8,128)} fusion(bf16[64,37,4608]{2,0,1:T(8,128)(2,1)} %constant_dynamic-update-slice_fusion, bf16[37]{0:T(256)(128)(2,1)S(1)} %copy-done.71, f32[1536]{0:T(1024)S(1)} %copy-done.38, f32[1536]{0:T(1024)S(1)} %copy-done.25, f32[64,37]{0,1:T(8,128)S(1)} %copy-done.17, f32[64,37]{0,1:T(8,128)S(1)} %copy-done.12, ...), kind=kOutput, calls=%fused_computation.33 | convolution fusion | flops 33557250048 | bytes 57440840 | tf_op jit(solution)/shard_map/btd,bte->de/dot_general | solution.py:122
  2787.1 11.1 fusion.62
  2806.0 1216.6 %all-reduce.8.cloned.1.call-done = (f32[1536,4608]{1,0:T(8,128)}, f32[24,64,1536]{2,1,0:T(8,128)}, f32[1536,4096]{1,0:T(8,128)}, f32[1536,4096]{1,0:T(8,128)}, f32[4096,1536]{1,0:T(8,128)}) async-done(((f32[1536,4608]{1,0:T(8,128)}, f32[24,64,1536]{2,1,0:T(8,128)}, f32[1536,4096]{1,0:T(8,128)}, f32[1536,4096]{1,0:T(8,128)}, f32[4096,1536]{1,0:T(8,128)}), (f32[1536,4608]{1,0:T(8,128)}, ...) | async-done | bytes 113246224 | tf_op jit(solution)/shard_map/psum | solution.py:127
  4025.3 21.1 copy.171
  4053.3 17.4 copy.178
  4071.3 20.2 copy.180
  4095.0 8.9 copy.182
  (257 shorter events, 99.8 us)
Async XLA Ops:
  16.6 43.7 %copy-start.11 = (f32[64,37]{0,1:T(8,128)}, f32[64,37]{0,1:T(8,128)S(1)}, u32[]{:S(2)}) copy-start(f32[64,37]{0,1:T(8,128)S(1)} %broadcast_multiply_fusion.5) | copy-start | bytes 28420
  20.2 40.1 copy-start.16
  20.2 40.1 copy-start.24
  20.2 40.0 copy-start.37
  232.5 207.9 %all-to-all-start = ((bf16[8,2,589824]{2,1,0:T(2,128)(2,1)}), bf16[8,2,589824]{2,1,0:T(2,128)(2,1)}, u32[]{:S(2)}, u32[]{:S(2)}) async-start(bf16[8,2,589824]{2,1,0:T(2,128)(2,1)} %reshape.148), calls=%async_computation | async-start | bytes 37748736 | tf_op jit(solution)/shard_map/all_to_all | solution.py:54
  614.5 34.1 copy-start.72
  676.8 21.9 copy-start.61
  676.8 21.9 copy-start.62
  676.8 21.9 copy-start.63
  676.8 22.0 copy-start.64
  690.6 17.2 copy-start.65
  690.6 17.8 copy-start.35
  690.6 18.4 copy-start.36
  690.6 19.0 copy-start.66
  690.6 19.6 slice-start.14
  690.6 259.0 %all-to-all-start.1 = ((bf16[8,2,196608]{2,1,0:T(2,128)(2,1)}), bf16[8,2,196608]{2,1,0:T(2,128)(2,1)}, u32[]{:S(2)}, u32[]{:S(2)}) async-start(bf16[8,2,196608]{2,1,0:T(2,128)(2,1)} %reshape.150), calls=%async_computation.1 | async-start | bytes 12582912 | tf_op jit(solution)/shard_map/all_to_all | solution.py:59
  698.7 276.9 %copy-start.47 = (f32[1536]{0:T(1024)}, f32[1536]{0:T(1024)S(1)}, u32[]{:S(2)}) copy-start(f32[1536]{0:T(1024)S(1)} %convert_element_type.105) | copy-start | bytes 18436
  698.7 276.9 %copy-start.50 = (f32[1536]{0:T(1024)}, f32[1536]{0:T(1024)S(1)}, u32[]{:S(2)}) copy-start(f32[1536]{0:T(1024)S(1)} %convert_element_type.114) | copy-start | bytes 18436
  698.7 347.4 %copy-start.42 = (f32[1536]{0:T(1024)}, f32[1536]{0:T(1024)S(1)}, u32[]{:S(2)}) copy-start(f32[1536]{0:T(1024)S(1)} %convert_element_type.118) | copy-start | bytes 18436
  698.8 347.4 %copy-start.45 = (f32[1536]{0:T(1024)}, f32[1536]{0:T(1024)S(1)}, u32[]{:S(2)}) copy-start(f32[1536]{0:T(1024)S(1)} %convert_element_type.119) | copy-start | bytes 18436
  1001.0 45.2 %copy-start.18 = (f32[64,37]{0,1:T(8,128)}, f32[64,37]{0,1:T(8,128)S(1)}, u32[]{:S(2)}) copy-start(f32[64,37]{0,1:T(8,128)S(1)} %broadcast_multiply_fusion.4) | copy-start | bytes 28420
  1001.0 45.2 %slice-start.15 = ((s8[7274496]{0:T(1024)(128)(4,1)}), s8[4194304]{0:T(1024)(128)(4,1)S(1)}, s32[]{:S(2)}) async-start(s8[7274496]{0:T(1024)(128)(4,1)} %bitcast.201), calls=%async_computation.22 | async-start | bytes 8388608
  1006.3 39.9 copy-start.26
  1006.3 39.9 slice-start.16
  1046.2 37.3 copy-start.30
  1046.2 37.3 copy-start.31
  1046.2 37.3 copy-start.39
  1046.3 37.3 copy-start.67
  1161.1 39.0 copy-start.19
  1161.1 39.0 copy-start.27
  1161.1 39.0 copy-start.43
  1200.1 49.7 %copy-start.40 = (f32[1536]{0:T(1024)S(1)}, f32[1536]{0:T(1024)}, u32[]{:S(2)}) copy-start(f32[1536]{0:T(1024)} %convert_element_type.117) | copy-start | bytes 18436
  1200.1 49.7 %copy-start.48 = (f32[1536]{0:T(1024)S(1)}, f32[1536]{0:T(1024)}, u32[]{:S(2)}) copy-start(f32[1536]{0:T(1024)} %copy-done.47) | copy-start | bytes 18436
  1200.1 49.7 %copy-start.51 = (f32[1536]{0:T(1024)S(1)}, f32[1536]{0:T(1024)}, u32[]{:S(2)}) copy-start(f32[1536]{0:T(1024)} %copy-done.50) | copy-start | bytes 18436
  1200.1 49.6 %copy-start.52 = (f32[1536]{0:T(1024)S(1)}, f32[1536]{0:T(1024)}, u32[]{:S(2)}) copy-start(f32[1536]{0:T(1024)} %convert_element_type.124) | copy-start | bytes 18436
  1200.1 49.6 %copy-start.68 = (bf16[64,5,1536]{2,0,1:T(8,128)(2,1)S(1)}, bf16[64,5,1536]{2,0,1:T(8,128)(2,1)}, u32[]{:S(2)}) copy-start(bf16[64,5,1536]{2,0,1:T(8,128)(2,1)} %param.38) | copy-start | bytes 2949124
  1342.0 19.6 slice-start.13
  1356.1 72.7 %all-to-all-start.2 = ((bf16[8,2,196608]{2,1,0:T(2,128)(2,1)}), bf16[8,2,196608]{2,1,0:T(2,128)(2,1)}, u32[]{:S(2)}, u32[]{:S(2)}) async-start(bf16[8,2,196608]{2,1,0:T(2,128)(2,1)} %reshape.152), calls=%async_computation.2 | async-start | bytes 12582912 | tf_op jit(solution)/shard_map/all_to_all | solution.py:54
  1361.1 94.5 %copy-start.21 = (bf16[5]{0:T(256)(128)(2,1)}, bf16[5]{0:T(256)(128)(2,1)S(1)}, u32[]{:S(2)}) copy-start(bf16[5]{0:T(256)(128)(2,1)S(1)} %broadcast_in_dim.2) | copy-start | bytes 34
  1363.4 104.4 %copy-start.2 = (bf16[64,5,3,64]{1,3,2,0:T(8,128)(2,1)}, bf16[64,5,3,64]{1,3,2,0:T(8,128)(2,1)S(1)}, u32[]{:S(2)}) copy-start(bf16[64,5,3,64]{1,3,2,0:T(8,128)(2,1)S(1)} %copy.120) | copy-start | bytes 368644
  1467.8 33.8 copy-start.73
  1601.1 99.8 %copy-start.3 = (bf16[64,5,3,64]{1,3,2,0:T(8,128)(2,1)S(1)}, bf16[64,5,3,64]{1,3,2,0:T(8,128)(2,1)}, u32[]{:S(2)}) copy-start(bf16[64,5,3,64]{1,3,2,0:T(8,128)(2,1)} %copy-done.2) | copy-start | bytes 368644
  1867.4 596.1 %all-to-all-start.3 = ((bf16[8,2,589824]{2,1,0:T(2,128)(2,1)}), bf16[8,2,589824]{2,1,0:T(2,128)(2,1)}, u32[]{:S(2)}, u32[]{:S(2)}) async-start(bf16[8,2,589824]{2,1,0:T(2,128)(2,1)} %reshape.154), calls=%async_computation.3 | async-start | bytes 37748736 | tf_op jit(solution)/shard_map/all_to_all | solution.py:59
  1876.0 519.8 %all-gather.2.cloned.1.call-start = ((), (), s32[]{:S(2)}) async-start(), calls=%async_computation.4 | async-start | bytes 84934656 | tf_op jit(solution)/shard_map/all_gather | solution.py:58
  1876.7 21.9 copy-start.20
  1876.7 21.9 copy-start.28
  1876.8 21.9 copy-start.44
  1876.8 21.9 copy-start.46
  1898.6 88.4 %slice-start.4 = ((s8[9437184]{0:T(1024)(128)(4,1)}), s8[4194304]{0:T(1024)(128)(4,1)S(1)}, s32[]{:S(2)}) async-start(s8[9437184]{0:T(1024)(128)(4,1)} %bitcast.195), calls=%async_computation.11 | async-start | bytes 8388608
  1898.6 88.4 %slice-start.5 = ((s8[9437184]{0:T(1024)(128)(4,1)}), s8[4194304]{0:T(1024)(128)(4,1)S(1)}, s32[]{:S(2)}) async-start(s8[9437184]{0:T(1024)(128)(4,1)} %bitcast.195), calls=%async_computation.12 | async-start | bytes 8388608
  1942.8 44.3 %slice-start.6 = ((s8[9437184]{0:T(1024)(128)(4,1)}), s8[1048576]{0:T(1024)(128)(4,1)S(1)}, s32[]{:S(2)}) async-start(s8[9437184]{0:T(1024)(128)(4,1)} %bitcast.195), calls=%async_computation.13 | async-start | bytes 2097152
  1996.0 810.0 %all-reduce.6.cloned.1.call-start = ((), (), s32[]{:S(2)}) async-start(), calls=%async_computation.5 | async-start | bytes 237568 | tf_op jit(solution)/shard_map/psum | solution.py:127
  2645.6 16.9 copy-start.25
  2725.6 1297.1 %all-reduce.8.cloned.1.call-start = ((), (), s32[]{:S(2)}) async-start(), calls=%async_computation.6 | async-start | bytes 226492416 | tf_op jit(solution)/shard_map/psum | solution.py:127
  4025.3 21.1 copy-start.29
  4025.3 21.8 copy-start.4
  4053.3 17.4 copy-start.33
  4070.6 21.4 slice-start.7
  4071.2 20.2 copy-start.32
  4071.2 20.8 slice-start.8
  4071.3 20.8 slice-start.9
  4071.3 21.3 slice-start.10
  4071.3 22.6 slice-start.11
  4071.3 23.7 slice-start.12
  (34 other events, 352.3 us)
Sparse Core Ops, SparseCore 0:
  1996.2 399.5 all-gather.1
  2725.7 44.2 all-reduce.5
  2776.3 1246.3 all-reduce.7
where the time goes:
time: 4130 us; the launch traced here: 4110 us
  waiting for transfers between devices  1820 us (44%)
  matrix products  990 us (24%)
  local copies, waits for them, and re-layouts  958 us (23%)
  blocking collectives  218 us (5%)
  other arithmetic  85.1 us (2%)
    psum x2, waiting for transfers between devices, local_block(): lax.psum((g_norm1_w, g_norm1_b, g_w_qkv, g_b_qkv, g_w_out, g_b_out, g_sca...  1220 us
    unnamed x210, local copies, waits for them, and re-layouts  454 us
    all_gather x1, waiting for transfers between devices, from_heads(): lax.all_gather(head_arr[:, :SPECIAL], 'sp', axis=head_axis, tiled=True)  355 us
    all_to_all x2, waiting for transfers between devices, to_heads(): lax.all_to_all(local_arr[:, SPECIAL:], 'sp', head_axis, 1, tiled=True)  248 us
    all_gather x1, blocking collectives, from_heads(): lax.all_gather(head_arr[:, :SPECIAL], 'sp', axis=head_axis, tiled=True)  218 us
    concatenate x4, local copies, waits for them, and re-layouts, from_heads(): return jnp.concatenate([spec_part, patch_part], axis=1)  147 us
    dot_general x1, matrix products, local_block(): jnp.einsum('bhqk,bqhd->bkhd', d_scores, queries, preferred_element_type=j...  99.8 us
    dot_general x1, matrix products, local_block(): jnp.einsum('bhqk,bkhd->bqhd', d_scores, key_vecs, preferred_element_type=...  99.5 us
  transfers between devices with their start and end apart: 7, of which 4 were waited for; matrix products, arithmetic and copies ran while one was open for 9% of the time, Pallas kernels for 0%

commit v1 on v0

v1 whole, which is shorter than its diff:
```python
import functools

import jax
import jax.numpy as jnp
from jax import lax
from jax.experimental import pallas as pl
from jax.experimental.pallas import tpu as pltpu
from jax.sharding import PartitionSpec as P

NORM_EPS = 1e-6
SPECIAL = 5
PAD_SPECIAL = 8
LANES = 128
F32 = jnp.float32
BF16 = jnp.bfloat16


def norm_forward(tok_f32, weight, bias):
    row_mean = jnp.mean(tok_f32, axis=-1, keepdims=True)
    centred = tok_f32 - row_mean
    inv_std = lax.rsqrt(jnp.mean(centred * centred, axis=-1, keepdims=True) + NORM_EPS)
    norm_hat = centred * inv_std
    normed = (norm_hat * weight.astype(F32) + bias.astype(F32)).astype(BF16)
    return norm_hat, inv_std, normed


def norm_backward(d_normed, norm_hat, inv_std, weight):
    d_hat = d_normed * weight.astype(F32)
    mean_grad = jnp.mean(d_hat, axis=-1, keepdims=True)
    mean_proj = jnp.mean(d_hat * norm_hat, axis=-1, keepdims=True)
    return inv_std * (d_hat - mean_grad - norm_hat * mean_proj)


def dot(lhs, rhs, lhs_dim, rhs_dim):
    return lax.dot_general(lhs, rhs, (((lhs_dim,), (rhs_dim,)), ((), ())), preferred_element_type=F32)


def softmax_rows(scores, real_keys, scale):
    col = lax.broadcasted_iota(jnp.int32, scores.shape, 1)
    scores = jnp.where(col < real_keys, scores, -jnp.inf)
    row_max = jnp.max(scores, axis=1, keepdims=True)
    weights = jnp.exp((scores - row_max) * scale)
    return weights / jnp.sum(weights, axis=1, keepdims=True)


def pair_slices(ref, pair, model_width):
    return [ref[0, :, pl.ds(pl.multiple_of(part * model_width + pair * LANES, LANES), LANES)] for part in range(3)]


def attn_fwd_kernel(real_keys, head_dim, qkv_ref, ctx_ref):
    model_width = ctx_ref.shape[2]
    scale = head_dim ** -0.5

    def body(pair, carry):
        q_two, k_two, v_two = pair_slices(qkv_ref, pair, model_width)
        low = lax.broadcasted_iota(jnp.int32, q_two.shape, 1) < head_dim
        zero = jnp.zeros_like(q_two)
        parts = []
        for half in range(2):
            q_one = jnp.where(low, q_two, zero) if half == 0 else jnp.where(low, zero, q_two)
            probs = softmax_rows(dot(q_one, k_two, 1, 1), real_keys, scale).astype(BF16)
            parts.append(dot(probs, v_two, 1, 0))
        col = pl.multiple_of(pair * LANES, LANES)
        ctx_ref[0, :, pl.ds(col, LANES)] = jnp.where(low, parts[0], parts[1]).astype(BF16)
        return carry

    lax.fori_loop(0, model_width // LANES, body, 0)


def attn_bwd_kernel(real_keys, head_dim, qkv_ref, dctx_ref, dqkv_ref):
    model_width = dctx_ref.shape[2]
    scale = head_dim ** -0.5

    def body(pair, carry):
        q_two, k_two, v_two = pair_slices(qkv_ref, pair, model_width)
        col = pl.multiple_of(pair * LANES, LANES)
        do_two = dctx_ref[0, :, pl.ds(col, LANES)]
        low = lax.broadcasted_iota(jnp.int32, q_two.shape, 1) < head_dim
        zero = jnp.zeros_like(q_two)
        dq, dk, dv = [], [], []
        for half in range(2):
            q_one = jnp.where(low, q_two, zero) if half == 0 else jnp.where(low, zero, q_two)
            do_one = jnp.where(low, do_two, zero) if half == 0 else jnp.where(low, zero, do_two)
            probs = softmax_rows(dot(q_one, k_two, 1, 1), real_keys, scale)
            d_probs = dot(do_one, v_two, 1, 1)
            inner = jnp.sum(d_probs * probs, axis=1, keepdims=True)
            d_scores = (probs * (d_probs - inner) * scale).astype(BF16)
            dv.append(dot(probs.astype(BF16), do_two, 0, 0))
            dq.append(dot(d_scores, k_two, 1, 0))
            dk.append(dot(d_scores, q_two, 0, 0))
        for part, pieces in enumerate((dq, dk, dv)):
            start = pl.multiple_of(part * model_width + pair * LANES, LANES)
            dqkv_ref[0, :, pl.ds(start, LANES)] = jnp.where(low, pieces[0], pieces[1]).astype(BF16)
        return carry

    lax.fori_loop(0, model_width // LANES, body, 0)


def row_block(rows, width):
    return pl.BlockSpec((1, rows, width), lambda image: (image, 0, 0))


def attn_cost(images, rows, width, head_dim, products):
    heads = width // head_dim
    return pl.CostEstimate(flops=2 * products * images * heads * rows * rows * 4 * head_dim,
                           bytes_accessed=images * rows * width * 2 * (4 if products == 2 else 7),
                           transcendentals=images * heads * rows * rows)


def attn_forward(qkv, real_keys, head_dim):
    images, rows, width3 = qkv.shape
    width = width3 // 3
    return pl.pallas_call(
        functools.partial(attn_fwd_kernel, real_keys, head_dim),
        out_shape=jax.ShapeDtypeStruct((images, rows, width), BF16),
        grid=(images,),
        in_specs=[row_block(rows, width3)],
        out_specs=row_block(rows, width),
        compiler_params=pltpu.CompilerParams(vmem_limit_bytes=60 * 2**20),
        cost_estimate=attn_cost(images, rows, width, head_dim, 2),
        name="attn_fwd",
    )(qkv)


def attn_backward(qkv, d_ctx, real_keys, head_dim):
    images, rows, width3 = qkv.shape
    width = width3 // 3
    return pl.pallas_call(
        functools.partial(attn_bwd_kernel, real_keys, head_dim),
        out_shape=jax.ShapeDtypeStruct((images, rows, width3), BF16),
        grid=(images,),
        in_specs=[row_block(rows, width3), row_block(rows, width)],
        out_specs=row_block(rows, width3),
        compiler_params=pltpu.CompilerParams(vmem_limit_bytes=60 * 2**20),
        cost_estimate=attn_cost(images, rows, width, head_dim, 5),
        name="attn_bwd",
    )(qkv, d_ctx)


def solution(mesh):
    groups = mesh.shape["sp"]
    tok_spec = P("dp", None, None)
    seq_spec = P("dp", "sp", None)
    shared = P()
    vec_spec = P("dp")
    mat_spec = P("dp", None)

    def local_block(spec_tok, patch_tok, norm1_w, norm1_b, w_qkv, b_qkv, w_out, b_out, scale_attn,
                    norm2_w, norm2_b, w_gate, b_gate, w_up, b_up, w_down, b_down, scale_mlp,
                    dy_spec, dy_patch):
        num_heads, head_dim, width = w_out.shape
        batch, local_patch = patch_tok.shape[0], patch_tok.shape[1]
        images = batch // groups
        patches = groups * local_patch
        rows = patches + PAD_SPECIAL
        real_rows = patches + SPECIAL
        total = images * rows
        rank = lax.axis_index("sp")

        def to_images(special, patch):
            sent = patch.reshape(groups, images, local_patch, width)
            got = lax.all_to_all(sent, "sp", 0, 0, tiled=True)
            got = jnp.transpose(got, (1, 0, 2, 3)).reshape(images, patches, width)
            own = lax.dynamic_slice_in_dim(special, rank * images, images, axis=0)
            own = jnp.pad(own, ((0, 0), (0, PAD_SPECIAL - SPECIAL), (0, 0)))
            return jnp.concatenate([got, own], axis=1).reshape(total, width)

        def from_images(value):
            value = value.reshape(images, rows, width)
            sent = jnp.transpose(value[:, :patches].reshape(images, groups, local_patch, width), (1, 0, 2, 3))
            patch = lax.all_to_all(sent, "sp", 0, 0, tiled=True).reshape(batch, local_patch, width)
            special = lax.all_gather(value[:, patches:real_rows], "sp", axis=0, tiled=True)
            return special, patch

        def col_sum(value):
            return jnp.sum(value, axis=0)

        tok_f32 = to_images(spec_tok, patch_tok).astype(F32)
        d_out = to_images(dy_spec, dy_patch).astype(F32)
        norm_hat1, inv_std1, normed1 = norm_forward(tok_f32, norm1_w, norm1_b)
        qkv = (dot(normed1, w_qkv, 1, 0) + b_qkv.astype(F32)).astype(BF16)
        qkv3 = qkv.reshape(images, rows, 3 * width)
        ctx = attn_forward(qkv3, real_rows, head_dim).reshape(total, width)
        w_out2 = w_out.reshape(width, width)
        branch1 = dot(ctx, w_out2, 1, 0) + b_out.astype(F32)
        resid_f32 = (tok_f32 + scale_attn.astype(F32) * branch1).astype(BF16).astype(F32)
        norm_hat2, inv_std2, normed2 = norm_forward(resid_f32, norm2_w, norm2_b)
        gate_pre = dot(normed2, w_gate, 1, 0) + b_gate.astype(F32)
        up_proj = dot(normed2, w_up, 1, 0) + b_up.astype(F32)
        gate_sig = jax.nn.sigmoid(gate_pre)
        gate_act = gate_pre * gate_sig
        hidden = (gate_act * up_proj).astype(BF16)
        branch2 = dot(hidden, w_down, 1, 0) + b_down.astype(F32)
        block_out = (resid_f32 + scale_mlp.astype(F32) * branch2).astype(BF16)

        g_scale_mlp = col_sum(d_out * branch2)
        d_branch2 = d_out * scale_mlp.astype(F32)
        g_b_down = col_sum(d_branch2)
        d_branch2_h = d_branch2.astype(BF16)
        g_w_down = dot(hidden, d_branch2_h, 0, 0)
        d_hidden = dot(d_branch2_h, w_down, 1, 1)
        d_up = d_hidden * gate_act
        d_gate = d_hidden * up_proj * gate_sig * (1.0 + gate_pre * (1.0 - gate_sig))
        g_b_gate = col_sum(d_gate)
        g_b_up = col_sum(d_up)
        d_gate_h = d_gate.astype(BF16)
        d_up_h = d_up.astype(BF16)
        g_w_gate = dot(normed2, d_gate_h, 0, 0)
        g_w_up = dot(normed2, d_up_h, 0, 0)
        d_normed2 = dot(d_gate_h, w_gate, 1, 1) + dot(d_up_h, w_up, 1, 1)
        g_norm2_w = col_sum(d_normed2 * norm_hat2)
        g_norm2_b = col_sum(d_normed2)
        d_resid = d_out + norm_backward(d_normed2, norm_hat2, inv_std2, norm2_w)
        g_scale_attn = col_sum(d_resid * branch1)
        d_branch1 = d_resid * scale_attn.astype(F32)
        g_b_out = col_sum(d_branch1)
        d_branch1_h = d_branch1.astype(BF16)
        g_w_out = dot(ctx, d_branch1_h, 0, 0).reshape(num_heads, head_dim, width)
        d_ctx = dot(d_branch1_h, w_out2, 1, 1).astype(BF16)
        d_qkv = attn_backward(qkv3, d_ctx.reshape(images, rows, width), real_rows, head_dim).reshape(total, 3 * width)
        g_b_qkv = col_sum(d_qkv.astype(F32))
        g_w_qkv = dot(normed1, d_qkv, 0, 0)
        d_normed1 = dot(d_qkv, w_qkv, 1, 1)
        g_norm1_w = col_sum(d_normed1 * norm_hat1)
        g_norm1_b = col_sum(d_normed1)
        d_tokens = (d_resid + norm_backward(d_normed1, norm_hat1, inv_std1, norm1_w)).astype(BF16)
        out_spec, out_patch = from_images(block_out)
        grad_spec, grad_patch = from_images(d_tokens)
        all_grads = lax.psum((g_norm1_w, g_norm1_b, g_w_qkv, g_b_qkv, g_w_out, g_b_out, g_scale_attn,
                              g_norm2_w, g_norm2_b, g_w_gate, g_b_gate, g_w_up, g_b_up, g_w_down, g_b_down,
                              g_scale_mlp), "sp")
        return (out_spec, out_patch, grad_spec, grad_patch) + all_grads

    in_specs = (tok_spec, seq_spec) + (shared,) * 16 + (tok_spec, seq_spec)
    out_specs = (tok_spec, seq_spec, tok_spec, seq_spec, vec_spec, vec_spec, mat_spec, vec_spec,
                 P("dp", None, None), vec_spec, vec_spec, vec_spec, vec_spec, mat_spec, vec_spec,
                 mat_spec, vec_spec, mat_spec, vec_spec, vec_spec)
    return jax.shard_map(local_block, mesh=mesh, in_specs=in_specs, out_specs=out_specs, check_vma=False)
```

time: 4130 us -> 2540 us (0.62)
  local copies, waits for them, and re-layouts: 958 us -> 132 us
  waiting for transfers between devices: 1820 us -> 1250 us
  matrix products: 990 us -> 547 us
  Pallas kernels: 0 us -> 280 us
    dot_general x31 -> x15, matrix products: 953 us -> 547 us  [dot(): lax.dot_general(lhs, rhs, (((lhs_dim,), (rhs_dim,)), ((), ())), preferred...]
    all_gather x1 -> x0, waiting for transfers between devices: 355 us -> none  [from_heads(): lax.all_gather(head_arr[:, :SPECIAL], 'sp', axis=head_axis, tiled=True)]
    unnamed x210 -> x170, local copies, waits for them, and re-layouts: 454 us -> 102 us
    pallas_call x0 -> x2, Pallas kernels: none -> 280 us  [the longest x1 172 us: attn_backward(): pl.pallas_call(functools.partial(attn_bwd_kernel, real_keys, head_dim), o...]
    concatenate x4 -> x0, local copies, waits for them, and re-layouts: 147 us -> none  [from_heads(): return jnp.concatenate([spec_part, patch_part], axis=1)]
    slice x13 -> x4, local copies, waits for them, and re-layouts: 120 us -> 5.96 us  [the longest x2 4.08 us: from_images(): value[:, :patches].reshape(images, groups, local_patch, width)]
    all_to_all x4 -> x3, waiting for transfers between devices: 248 us -> 136 us  [the longest x2 85.5 us: from_images(): lax.all_to_all(sent, 'sp', 0, 0, tiled=True)]
    all_to_all x5 -> x0, local copies, waits for them, and re-layouts: 98.3 us -> none  [the longest x4 85.7 us: to_heads(): lax.all_to_all(local_arr[:, SPECIAL:], 'sp', head_axis, 1, tiled=True)]
  transfers between devices with their start and end apart: 7 -> 5, of which waited for: 4 -> 3; matrix products, arithmetic and copies ran while one was open for 9% -> 2% of each run, Pallas kernels for 0% -> 0%
where the time goes in v1:
time: 2540 us; the launch traced here: 2530 us
  waiting for transfers between devices  1250 us (49%)
  matrix products  547 us (22%)
  Pallas kernels  280 us (11%)
  blocking collectives  237 us (9%)
  local copies, waits for them, and re-layouts  132 us (5%)
  other arithmetic  44.2 us (2%)
    psum x2, waiting for transfers between devices, local_block(): lax.psum((g_norm1_w, g_norm1_b, g_w_qkv, g_b_qkv, g_w_out, g_b_out, g_sca...  1120 us
    dot_general x15, matrix products, dot(): lax.dot_general(lhs, rhs, (((lhs_dim,), (rhs_dim,)), ((), ())), preferred...  547 us
    pallas_call x1, Pallas kernels, attn_backward(): pl.pallas_call(functools.partial(attn_bwd_kernel, real_keys, head_dim), o...  172 us
    all_gather x2, blocking collectives, from_images(): lax.all_gather(value[:, patches:real_rows], 'sp', axis=0, tiled=True)  163 us
    pallas_call x1, Pallas kernels, attn_forward(): pl.pallas_call(functools.partial(attn_fwd_kernel, real_keys, head_dim), o...  108 us
    unnamed x170, local copies, waits for them, and re-layouts  102 us
    all_to_all x2, waiting for transfers between devices, from_images(): lax.all_to_all(sent, 'sp', 0, 0, tiled=True)  85.5 us
    all_to_all x1, blocking collectives, to_images(): got = lax.all_to_all(sent, 'sp', 0, 0, tiled=True)  75 us
  transfers between devices with their start and end apart: 5, of which 3 were waited for; matrix products, arithmetic and copies ran while one was open for 2% of the time, Pallas kernels for 0%

profile of v1, /device:TPU:1, one launch (start us, length us, event | category | flops | bytes accessed | tf_op | source)
XLA Modules:
  0.0 2528.3 jit_solution(15891302130566121984)
XLA Ops:
  7.3 75.0 %all_to_all.20 = bf16[8,8,32,1536]{3,2,1,0:T(8,128)(2,1)} all-to-all(bf16[8,8,32,1536]{3,2,1,0:T(8,128)(2,1)} %bitcast.98), channel_id=1, replica_groups=mesh['dp'=1,'sp'=8] {'sp'}, dimensions={0} | all-to-all | bytes 12582912 | tf_op jit(solution)/shard_map/all_to_all | solution.py:162
  82.3 4.6 all-to-all-start.2
  86.9 0.6 convert_element_type.119
  88.8 0.6 convert_element_type.122
  89.5 0.6 convert_element_type.123
  90.2 1.0 constant_dynamic-slice_fusion
  91.2 3.6 copy.40
  94.8 2.7 copy-done.2
  97.5 1.5 convert_reduce_fusion.2
  99.1 4.7 fusion.23
  103.8 50.9 %all-to-all-done.2 = bf16[8,8,32,1536]{3,2,1,0:T(8,128)(2,1)} async-done(((bf16[8,8,32,1536]{3,2,1,0:T(8,128)(2,1)}), bf16[8,8,32,1536]{3,2,1,0:T(8,128)(2,1)}, u32[]{:S(2)}, u32[]{:S(2)}) %all-to-all-start.2) | async-done | bytes 6291488 | tf_op jit(solution)/shard_map/all_to_all | solution.py:162
  154.7 3.5 copy.44
  158.2 2.7 fusion.18
  160.9 3.8 fusion.19
  164.8 4.4 fusion.27
  169.3 38.3 %add_convert_fusion = bf16[2112,4608]{1,0:T(8,128)(2,1)} fusion(bf16[1536,4608]{1,0:T(8,128)(2,1)} %param.24, f32[4608]{0:T(1024)S(1)} %convert_element_type.113, f32[2112,1536]{1,0:T(8,128)S(1)} %fusion.27, f32[1536]{0:T(1024)S(1)} %convert_element_type.111, f32[1536]{0:T(1024)S(1)} %convert_element_type.110), kind=kOutput, calls=%fused_computation.1 | convolution fusion | flops 29926195200 | bytes 46626816 | tf_op jit(solution)/shard_map/dot_general | solution.py:35
  207.6 108.2 %attn_fwd.1 = bf16[8,264,1536]{2,1,0:T(8,128)(2,1)} custom-call(bf16[8,264,4608]{2,1,0:T(8,128)(2,1)} %bitcast.102), custom_call_target="tpu_custom_call" | custom-call | flops 13702791168 | bytes 25952256 | tf_op jit(solution)/shard_map/attn_fwd/pallas_call | solution.py:113
  315.8 17.9 bitcast_add_fusion
  333.7 0.9 convert_reduce_fusion.1
  334.6 1.8 fusion.14
  336.5 33.9 %fusion.47 = f32[2112,4096]{1,0:T(8,128)} fusion(bf16[1536,4096]{1,0:T(8,128)(2,1)} %param.33, bf16[2112,1536]{1,0:T(8,128)(2,1)S(1)} %get-tuple-element.62, f32[1536]{0:T(1024)S(1)} %copy-done.43, f32[1536]{0:T(1024)S(1)} %copy-done.41, f32[2112]{0:T(1024)S(1)} %add_rsqrt_fusion, f32[2112]{0:T(1024)S(1)} %broadcast_multiply_fusion.4), kind=kOutput, calls=%fused_computation.87 | convolution fusion | flops 26594574336 | bytes 53703168 | tf_op jit(solution)/shard_map/dot_general | solution.py:35
  370.5 34.3 %fusion.49 = f32[2112,4096]{1,0:T(8,128)} fusion(bf16[1536,4096]{1,0:T(8,128)(2,1)} %param.31, bf16[2112,1536]{1,0:T(8,128)(2,1)S(1)} %get-tuple-element.62, f32[1536]{0:T(1024)S(1)} %copy-done.43, f32[1536]{0:T(1024)S(1)} %copy-done.41, f32[2112]{0:T(1024)S(1)} %add_rsqrt_fusion, f32[2112]{0:T(1024)S(1)} %broadcast_multiply_fusion.4), kind=kOutput, calls=%fused_computation.88 | convolution fusion | flops 26594574336 | bytes 53703168 | tf_op jit(solution)/shard_map/dot_general | solution.py:35
  404.8 56.7 %multiply_reduce_fusion = (f32[4096]{0:T(1024)}, bf16[2112,4096]{1,0:T(8,128)(2,1)}, bf16[2112,4096]{1,0:T(8,128)(2,1)}, f32[4096]{0:T(1024)}, bf16[2112,4096]{1,0:T(8,128)(2,1)}) fusion(f32[2112,4096]{1,0:T(8,128)} %fusion.49, f32[4096]{0:T(1024)S(1)} %copy-done.29, f32[2112,4096]{1,0:T(8,128)} %fusion.47, f32[4096]{0:T(1024)S(1)} %copy-done.30, ...), kind=kOutput, calls=%fused_computation.16 | convolution fusion | flops 26739466240 | bytes 140247040 | tf_op jit(solution)/shard_map/dot_general | solution.py:35
  461.6 35.4 %fusion.30 = f32[2112,1536]{1,0:T(8,128)} fusion(bf16[1536,4096]{1,0:T(8,128)(2,1)} %param.31, bf16[2112,4096]{1,0:T(8,128)(2,1)} %get-tuple-element.56), kind=kOutput, calls=%fused_computation.62 | convolution fusion | flops 26575110144 | bytes 42860544 | tf_op jit(solution)/shard_map/dot_general | solution.py:35
  497.0 37.9 %fusion.54 = f32[4096,1536]{1,0:T(8,128)} fusion(bf16[2112,4096]{1,0:T(8,128)(2,1)} %get-tuple-element.54, bf16[2112,1536]{1,0:T(8,128)(2,1)} %fusion.19), kind=kOutput, calls=%fused_computation.91 | convolution fusion | flops 26575110144 | bytes 48955392 | tf_op jit(solution)/shard_map/dot_general | solution.py:35
  534.9 43.2 %fusion.13 = (f32[1536]{0:T(1024)}, f32[2112]{0:T(1024)S(1)}, f32[2112]{0:T(1024)S(1)}, f32[1536]{0:T(1024)}, f32[2112,1536]{1,0:T(8,128)}) fusion(bf16[2112,1536]{1,0:T(8,128)(2,1)S(1)} %copy-done.6, f32[2112]{0:T(1024)S(1)} %copy-done.34, f32[2112]{0:T(1024)S(1)} %copy-done.23, f32[1536]{0:T(1024)S(1)} %copy-done.42, f32[2112,1536]{1,0:T(8,128)} %fusion.30, ...), kind=kOutput, calls=%fused_computation.27 | convolution fusion | flops 26610786304 | bytes 62376960 | tf_op jit(solution)/shard_map/dot_general | solution.py:35
  578.2 44.7 %fusion.20 = (f32[1536]{0:T(1024)}, bf16[2112,1536]{1,0:T(8,128)(2,1)}, f32[1536]{0:T(1024)}, f32[1536]{0:T(1024)}, f32[2112,1536]{1,0:T(8,128)}) fusion(bf16[8,5,1536]{2,1,0:T(8,128)(2,1)S(1)} %copy-done.13, bf16[8,256,1536]{2,1,0:T(8,128)(2,1)} %bitcast.80, f32[1536]{0:T(1024)S(1)} %copy-done.21, bf16[2112,1536]{1,0:T(8,128)(2,1)} %copy-done.5, ...), kind=kOutput, calls=%fused_computation.38 | convolution fusion | flops 26656204800 | bytes 88280064 | tf_op jit(solution)/shard_map/dot_general | solution.py:35
  622.9 16.4 convolution_convert_fusion
  639.3 172.0 %attn_bwd.1 = bf16[8,264,4608]{2,1,0:T(8,128)(2,1)} custom-call(bf16[8,264,4608]{2,1,0:T(8,128)(2,1)} %bitcast.103, bf16[8,264,1536]{2,1,0:T(8,128)(2,1)} %bitcast.104), custom_call_target="tpu_custom_call" | custom-call | flops 34256977920 | bytes 45416448 | tf_op jit(solution)/shard_map/attn_bwd/pallas_call | solution.py:128
  811.3 9.7 convert_reduce_fusion
  821.1 42.5 %convolution_bitcast_fusion = f32[1536,4608]{1,0:T(8,128)} fusion(bf16[8,264,4608]{2,1,0:T(8,128)(2,1)} %attn_bwd.1, f32[1536]{0:T(1024)S(1)} %copy-done.46, f32[1536]{0:T(1024)S(1)} %copy-done.27, f32[8,264]{1,0:T(8,128)S(1)} %copy-done.25, f32[8,264]{1,0:T(8,128)S(1)} %copy-done.19, bf16[8,5,1536]{2,1,0:T(8,128)(2,1)S(1)} %copy-done.11, ...), kind=kOutput, calls=%fused_computation.6 | convolution fusion | flops 29932683264 | bytes 54219264 | tf_op jit(solution)/shard_map/dot_general | solution.py:35
  863.6 39.9 %fusion.44 = f32[1536,4096]{1,0:T(8,128)} fusion(bf16[2112,4096]{1,0:T(8,128)(2,1)} %get-tuple-element.53, bf16[2112,1536]{1,0:T(8,128)(2,1)} %copy-done.5, f32[1536]{0:T(1024)S(1)} %copy-done.44, f32[1536]{0:T(1024)S(1)} %copy-done.42, f32[2112]{0:T(1024)S(1)} %copy-done.34, f32[2112]{0:T(1024)S(1)} %copy-done.23), kind=kOutput, calls=%fused_computation.86 | convolution fusion | flops 26594574336 | bytes 48984576 | tf_op jit(solution)/shard_map/dot_general | solution.py:35
  903.5 39.9 %fusion.28 = f32[1536,4096]{1,0:T(8,128)} fusion(bf16[2112,4096]{1,0:T(8,128)(2,1)} %get-tuple-element.56, bf16[2112,1536]{1,0:T(8,128)(2,1)} %copy-done.5, f32[1536]{0:T(1024)S(1)} %copy-done.44, f32[1536]{0:T(1024)S(1)} %copy-done.42, f32[2112]{0:T(1024)S(1)} %copy-done.34, f32[2112]{0:T(1024)S(1)} %copy-done.23), kind=kOutput, calls=%fused_computation.60 | convolution fusion | flops 26594574336 | bytes 48984576 | tf_op jit(solution)/shard_map/dot_general | solution.py:35
  943.5 9.3 copy.48
  952.8 47.1 %fusion.51 = (f32[1536]{0:T(1024)}, f32[1536]{0:T(1024)}, f32[2112]{0:T(1024)S(1)}, f32[2112]{0:T(1024)S(1)}, f32[2112,1536]{1,0:T(8,128)}) fusion(f32[2112]{0:T(1024)S(1)} %copy-done.17, f32[2112]{0:T(1024)S(1)} %copy-done.15, bf16[8,5,1536]{2,1,0:T(8,128)(2,1)S(1)} %copy-done.11, bf16[8,256,1536]{2,1,0:T(8,128)(2,1)} %bitcast.75, ...), kind=kOutput, calls=%fused_computation.89 | convolution fusion | flops 29945651200 | bytes 66038784 | tf_op jit(solution)/shard_map/dot_general | solution.py:35
  999.9 18.5 fusion.35
  1018.4 3.5 slice.17
  1021.9 3.4 copy.56
  1025.3 7.6 all-to-all-start.1
  1032.9 11.6 add_convert_fusion.1
  1044.6 2.6 copy-done.7
  1047.2 0.6 slice.19
  1047.8 3.4 copy.55
  1051.3 85.5 %all-to-all-done.1 = bf16[8,8,32,1536]{3,2,1,0:T(8,128)(2,1)} async-done(((bf16[8,8,32,1536]{3,2,1,0:T(8,128)(2,1)}), bf16[8,8,32,1536]{3,2,1,0:T(8,128)(2,1)}, u32[]{:S(2)}, u32[]{:S(2)}) %all-to-all-start.1) | async-done | bytes 6291488 | tf_op jit(solution)/shard_map/all_to_all | solution.py:171
  1136.7 5.0 all-to-all-start.3
  1141.7 0.9 slice.16
  1142.7 0.9 slice.18
  1143.7 142.3 %all_gather.6 = bf16[64,5,1536]{2,0,1:T(8,128)(2,1)S(1)} all-gather(bf16[8,5,1536]{2,0,1:T(8,128)(2,1)S(1)} %copy.49), channel_id=1, replica_groups=mesh['dp'=1,'sp'=8] {'sp'}, dimensions={0}, use_global_device_ids=true | all-gather | bytes 1105920 | tf_op jit(solution)/shard_map/all_gather | solution.py:172
  1286.1 20.2 all_gather.7
  1306.3 1118.5 %all-reduce.9.cloned.1.call-done = (f32[1536,4608]{1,0:T(8,128)}, f32[24,64,1536]{2,1,0:T(8,128)}, f32[1536,4096]{1,0:T(8,128)}, f32[1536,4096]{1,0:T(8,128)}, f32[4096,1536]{1,0:T(8,128)}) async-done(((f32[1536,4608]{1,0:T(8,128)}, f32[24,64,1536]{2,1,0:T(8,128)}, f32[1536,4096]{1,0:T(8,128)}, f32[1536,4096]{1,0:T(8,128)}, f32[4096,1536]{1,0:T(8,128)}), (f32[1536,4608]{1,0:T(8,128)}, ...) | async-done | bytes 113246224 | tf_op jit(solution)/shard_map/psum | solution.py:229
  2424.8 0.9 copy.77
  2425.7 6.3 copy.78
  2432.0 0.9 copy.79
  2432.9 6.4 copy.80
  2440.5 21.7 copy.83
  2462.3 0.6 copy.84
  2462.9 3.7 copy.85
  2469.0 17.4 copy.90
  2486.4 0.6 copy.91
  2487.1 20.2 copy.92
  2507.2 0.6 copy.93
  2508.4 1.2 slice-done.4
  2509.6 1.2 slice-done.5
  2510.8 8.9 copy.94
  (180 shorter events, 7.4 us)
Async XLA Ops:
  7.2 82.9 %copy-start = (bf16[64,5,1536]{2,0,1:T(8,128)(2,1)S(1)}, bf16[64,5,1536]{2,0,1:T(8,128)(2,1)}, u32[]{:S(2)}) copy-start(bf16[64,5,1536]{2,0,1:T(8,128)(2,1)} %param.20) | copy-start | bytes 2949124
  7.2 79.7 %copy-start.56 = (bf16[1536]{0:T(1024)(128)(2,1)S(1)}, bf16[1536]{0:T(1024)(128)(2,1)}, u32[]{:S(2)}) copy-start(bf16[1536]{0:T(1024)(128)(2,1)} %param.29) | copy-start | bytes 9220
  7.2 80.3 %copy-start.57 = (bf16[1536]{0:T(1024)(128)(2,1)S(1)}, bf16[1536]{0:T(1024)(128)(2,1)}, u32[]{:S(2)}) copy-start(bf16[1536]{0:T(1024)(128)(2,1)} %param.22) | copy-start | bytes 9220
  7.2 80.3 %copy-start.58 = (bf16[1536]{0:T(1024)(128)(2,1)S(1)}, bf16[1536]{0:T(1024)(128)(2,1)}, u32[]{:S(2)}) copy-start(bf16[1536]{0:T(1024)(128)(2,1)} %param.28) | copy-start | bytes 9220
  7.2 80.3 %copy-start.59 = (bf16[1536]{0:T(1024)(128)(2,1)S(1)}, bf16[1536]{0:T(1024)(128)(2,1)}, u32[]{:S(2)}) copy-start(bf16[1536]{0:T(1024)(128)(2,1)} %param.30) | copy-start | bytes 9220
  7.3 80.9 %copy-start.60 = (bf16[1536]{0:T(1024)(128)(2,1)S(1)}, bf16[1536]{0:T(1024)(128)(2,1)}, u32[]{:S(2)}) copy-start(bf16[1536]{0:T(1024)(128)(2,1)} %param.37) | copy-start | bytes 9220
  7.3 80.9 %copy-start.61 = (bf16[1536]{0:T(1024)(128)(2,1)S(1)}, bf16[1536]{0:T(1024)(128)(2,1)}, u32[]{:S(2)}) copy-start(bf16[1536]{0:T(1024)(128)(2,1)} %param.23) | copy-start | bytes 9220
  7.3 80.9 %copy-start.62 = (bf16[1536]{0:T(1024)(128)(2,1)S(1)}, bf16[1536]{0:T(1024)(128)(2,1)}, u32[]{:S(2)}) copy-start(bf16[1536]{0:T(1024)(128)(2,1)} %param.27) | copy-start | bytes 9220
  7.3 80.9 %copy-start.63 = (bf16[1536]{0:T(1024)(128)(2,1)S(1)}, bf16[1536]{0:T(1024)(128)(2,1)}, u32[]{:S(2)}) copy-start(bf16[1536]{0:T(1024)(128)(2,1)} %param.36) | copy-start | bytes 9220
  7.3 81.6 %copy-start.36 = (bf16[4096]{0:T(1024)(128)(2,1)S(1)}, bf16[4096]{0:T(1024)(128)(2,1)}, u32[]{:S(2)}) copy-start(bf16[4096]{0:T(1024)(128)(2,1)} %param.32) | copy-start | bytes 24580
  7.3 82.2 %copy-start.37 = (bf16[4096]{0:T(1024)(128)(2,1)S(1)}, bf16[4096]{0:T(1024)(128)(2,1)}, u32[]{:S(2)}) copy-start(bf16[4096]{0:T(1024)(128)(2,1)} %param.34) | copy-start | bytes 24580
  7.3 82.8 %copy-start.35 = (bf16[4608]{0:T(1024)(128)(2,1)S(1)}, bf16[4608]{0:T(1024)(128)(2,1)}, u32[]{:S(2)}) copy-start(bf16[4608]{0:T(1024)(128)(2,1)} %param.25) | copy-start | bytes 27652
  82.3 72.4 %all-to-all-start.2 = ((bf16[8,8,32,1536]{3,2,1,0:T(8,128)(2,1)}), bf16[8,8,32,1536]{3,2,1,0:T(8,128)(2,1)}, u32[]{:S(2)}, u32[]{:S(2)}) async-start(bf16[8,8,32,1536]{3,2,1,0:T(8,128)(2,1)} %bitcast.99), calls=%async_computation.2 | async-start | bytes 12582912 | tf_op jit(solution)/shard_map/all_to_all | solution.py:162
  86.9 1219.4 %all-reduce.7.cloned.1.call-start = ((), (), s32[]{:S(2)}) async-start(), calls=%async_computation.4 | async-start | bytes 237568 | tf_op jit(solution)/shard_map/psum | solution.py:229
  87.5 81.7 %copy-start.26 = (f32[1536]{0:T(1024)}, f32[1536]{0:T(1024)S(1)}, u32[]{:S(2)}) copy-start(f32[1536]{0:T(1024)S(1)} %convert_element_type.110) | copy-start | bytes 18436
  87.6 228.2 %copy-start.38 = (f32[1536]{0:T(1024)}, f32[1536]{0:T(1024)S(1)}, u32[]{:S(2)}) copy-start(f32[1536]{0:T(1024)S(1)} %convert_element_type.108) | copy-start | bytes 18436
  88.2 72.7 %copy-start.20 = (f32[1536]{0:T(1024)}, f32[1536]{0:T(1024)S(1)}, u32[]{:S(2)}) copy-start(f32[1536]{0:T(1024)S(1)} %convert_element_type.118) | copy-start | bytes 18436
  88.2 81.0 %copy-start.45 = (f32[1536]{0:T(1024)}, f32[1536]{0:T(1024)S(1)}, u32[]{:S(2)}) copy-start(f32[1536]{0:T(1024)S(1)} %convert_element_type.111) | copy-start | bytes 18436
  90.2 225.6 %copy-start.10 = (bf16[8,5,1536]{2,1,0:T(8,128)(2,1)}, bf16[8,5,1536]{2,1,0:T(8,128)(2,1)S(1)}, u32[]{:S(2)}) copy-start(bf16[8,5,1536]{2,1,0:T(8,128)(2,1)S(1)} %copy.51) | copy-start | bytes 368644
  91.2 69.6 %copy-start.12 = (bf16[8,5,1536]{2,1,0:T(8,128)(2,1)}, bf16[8,5,1536]{2,1,0:T(8,128)(2,1)S(1)}, u32[]{:S(2)}) copy-start(bf16[8,5,1536]{2,1,0:T(8,128)(2,1)S(1)} %copy.52) | copy-start | bytes 368644
  99.0 65.7 %copy-start.18 = (f32[8,264]{1,0:T(8,128)}, f32[8,264]{1,0:T(8,128)S(1)}, u32[]{:S(2)}) copy-start(f32[8,264]{1,0:T(8,128)S(1)} %broadcast_multiply_fusion.5) | copy-start | bytes 25348
  99.1 65.7 %copy-start.14 = (f32[2112]{0:T(1024)}, f32[2112]{0:T(1024)S(1)}, u32[]{:S(2)}) copy-start(f32[2112]{0:T(1024)S(1)} %div.30) | copy-start | bytes 25348
  164.7 42.8 %copy-start.24 = (f32[8,264]{1,0:T(8,128)}, f32[8,264]{1,0:T(8,128)S(1)}, u32[]{:S(2)}) copy-start(f32[8,264]{1,0:T(8,128)S(1)} %add_rsqrt_fusion.1) | copy-start | bytes 25348
  164.8 42.7 %copy-start.16 = (f32[2112]{0:T(1024)}, f32[2112]{0:T(1024)S(1)}, u32[]{:S(2)}) copy-start(f32[2112]{0:T(1024)S(1)} %rsqrt.21) | copy-start | bytes 25348
  169.3 38.3 %copy-start.8 = (f32[2112,1536]{1,0:T(8,128)}, f32[2112,1536]{1,0:T(8,128)S(1)}, u32[]{:S(2)}) copy-start(f32[2112,1536]{1,0:T(8,128)S(1)} %fusion.27) | copy-start | bytes 38928388
  333.6 36.8 %copy-start.5 = (bf16[2112,1536]{1,0:T(8,128)(2,1)}, bf16[2112,1536]{1,0:T(8,128)(2,1)S(1)}, u32[]{:S(2)}) copy-start(bf16[2112,1536]{1,0:T(8,128)(2,1)S(1)} %get-tuple-element.62) | copy-start | bytes 19464196
  334.6 35.9 %copy-start.22 = (f32[2112]{0:T(1024)}, f32[2112]{0:T(1024)S(1)}, u32[]{:S(2)}) copy-start(f32[2112]{0:T(1024)S(1)} %broadcast_multiply_fusion.4) | copy-start | bytes 25348
  336.5 34.0 %copy-start.33 = (f32[2112]{0:T(1024)}, f32[2112]{0:T(1024)S(1)}, u32[]{:S(2)}) copy-start(f32[2112]{0:T(1024)S(1)} %add_rsqrt_fusion) | copy-start | bytes 25348
  370.5 34.4 %copy-start.9 = (bf16[2112,1536]{1,0:T(8,128)(2,1)S(1)}, bf16[2112,1536]{1,0:T(8,128)(2,1)}, u32[]{:S(2)}) copy-start(bf16[2112,1536]{1,0:T(8,128)(2,1)} %fusion.19) | copy-start | bytes 19464196
  370.5 34.3 %copy-start.29 = (f32[4096]{0:T(1024)S(1)}, f32[4096]{0:T(1024)}, u32[]{:S(2)}) copy-start(f32[4096]{0:T(1024)} %convert_element_type.122) | copy-start | bytes 49156
  370.5 34.3 %copy-start.30 = (f32[4096]{0:T(1024)S(1)}, f32[4096]{0:T(1024)}, u32[]{:S(2)}) copy-start(f32[4096]{0:T(1024)} %convert_element_type.123) | copy-start | bytes 49156
  497.0 37.9 %copy-start.6 = (bf16[2112,1536]{1,0:T(8,128)(2,1)S(1)}, bf16[2112,1536]{1,0:T(8,128)(2,1)}, u32[]{:S(2)}) copy-start(bf16[2112,1536]{1,0:T(8,128)(2,1)} %copy-done.5) | copy-start | bytes 19464196
  497.0 37.9 %copy-start.23 = (f32[2112]{0:T(1024)S(1)}, f32[2112]{0:T(1024)}, u32[]{:S(2)}) copy-start(f32[2112]{0:T(1024)} %copy-done.22) | copy-start | bytes 25348
  497.0 37.9 %copy-start.34 = (f32[2112]{0:T(1024)S(1)}, f32[2112]{0:T(1024)}, u32[]{:S(2)}) copy-start(f32[2112]{0:T(1024)} %copy-done.33) | copy-start | bytes 25348
  497.0 37.9 %copy-start.42 = (f32[1536]{0:T(1024)S(1)}, f32[1536]{0:T(1024)}, u32[]{:S(2)}) copy-start(f32[1536]{0:T(1024)} %convert_element_type.119) | copy-start | bytes 18436
  534.9 43.3 %copy-start.13 = (bf16[8,5,1536]{2,1,0:T(8,128)(2,1)S(1)}, bf16[8,5,1536]{2,1,0:T(8,128)(2,1)}, u32[]{:S(2)}) copy-start(bf16[8,5,1536]{2,1,0:T(8,128)(2,1)} %copy-done.12) | copy-start | bytes 368644
  534.9 43.3 %copy-start.21 = (f32[1536]{0:T(1024)S(1)}, f32[1536]{0:T(1024)}, u32[]{:S(2)}) copy-start(f32[1536]{0:T(1024)} %copy-done.20) | copy-start | bytes 18436
  534.9 43.2 %copy-start.39 = (f32[1536]{0:T(1024)S(1)}, f32[1536]{0:T(1024)}, u32[]{:S(2)}) copy-start(f32[1536]{0:T(1024)} %copy-done.38) | copy-start | bytes 18436
  534.9 43.2 %copy-start.47 = (f32[1536]{0:T(1024)S(1)}, f32[1536]{0:T(1024)}, u32[]{:S(2)}) copy-start(f32[1536]{0:T(1024)} %convert_element_type.125) | copy-start | bytes 18436
  811.3 9.7 copy-start.3
  811.3 9.7 copy-start.11
  811.3 9.7 copy-start.19
  811.3 9.7 copy-start.25
  811.3 9.7 copy-start.27
  821.1 42.6 %copy-start.44 = (f32[1536]{0:T(1024)S(1)}, f32[1536]{0:T(1024)}, u32[]{:S(2)}) copy-start(f32[1536]{0:T(1024)} %convert_element_type.120) | copy-start | bytes 18436
  952.8 47.1 %copy-start.40 = (f32[1536]{0:T(1024)S(1)}, f32[1536]{0:T(1024)}, u32[]{:S(2)}) copy-start(f32[1536]{0:T(1024)} %copy-done.38) | copy-start | bytes 18436
  999.8 1424.9 %all-reduce.9.cloned.1.call-start = ((), (), s32[]{:S(2)}) async-start(), calls=%async_computation.5 | async-start | bytes 226492416 | tf_op jit(solution)/shard_map/psum | solution.py:229
  1025.3 111.4 %all-to-all-start.1 = ((bf16[8,8,32,1536]{3,2,1,0:T(8,128)(2,1)}), bf16[8,8,32,1536]{3,2,1,0:T(8,128)(2,1)}, u32[]{:S(2)}, u32[]{:S(2)}) async-start(bf16[8,8,32,1536]{3,2,1,0:T(8,128)(2,1)} %bitcast.86), calls=%async_computation.1 | async-start | bytes 12582912 | tf_op jit(solution)/shard_map/all_to_all | solution.py:171
  1136.7 169.5 %all-to-all-start.3 = ((bf16[8,8,32,1536]{3,2,1,0:T(8,128)(2,1)}), bf16[8,8,32,1536]{3,2,1,0:T(8,128)(2,1)}, u32[]{:S(2)}, u32[]{:S(2)}) async-start(bf16[8,8,32,1536]{3,2,1,0:T(8,128)(2,1)} %bitcast.87), calls=%async_computation.3 | async-start | bytes 12582912 | tf_op jit(solution)/shard_map/all_to_all | solution.py:171
  2425.7 13.6 copy-start.55
  2425.7 14.2 copy-start.54
  2432.9 29.9 %slice-start.6 = ((s8[9437184]{0:T(1024)(128)(4,1)}), s8[4194304]{0:T(1024)(128)(4,1)S(1)}, s32[]{:S(2)}) async-start(s8[9437184]{0:T(1024)(128)(4,1)} %bitcast.91), calls=%async_computation.12 | async-start | bytes 8388608
  2440.5 21.7 copy-start.28
  2440.5 22.3 slice-start.7
  2440.5 22.3 slice-start.8
  2469.0 17.4 copy-start.32
  2486.4 21.4 slice-start
  2487.0 20.2 copy-start.31
  2487.0 20.8 slice-start.1
  2487.0 20.8 slice-start.2
  2487.0 21.3 slice-start.3
  2487.0 22.6 slice-start.4
  2487.0 23.7 slice-start.5
  2507.2 13.7 copy-start.1
  (14 other events, 81.6 us)
Sparse Core Ops, SparseCore 0:
  1000.0 55.7 all-reduce.6
  1062.1 1362.6 all-reduce.8
